TPU v7x, 32 devices: a whole 2x2x4 slice. The times are simulated.
32 devices in a mesh: dp: 8 (over y, x, core), mp: 4 (over z).
Axes of the slice: x: 2, y: 2, z: 4, core: 2. Of those that a mesh axis runs over, the one named last changes fastest.
Arguments:
- vit_features: bfloat16 [32, 256, 1024], P('dp', 'mp'), may hold values from -6 to 6
- patch_counts: int32 [32], P('dp'), may hold values from 64 to 192
- text_counts: int32 [32], P('dp'), may hold values from 1 to 63
- tile_dest: int32 [32], P('dp'), may hold values from 0 to 7, as said below
- text_embeds: bfloat16 [32, 256, 4096], P('dp', 'mp'), may hold values from -6 to 6
- w_proj: bfloat16 [1024, 4096], replicated, may hold values from -0.1875 to 0.1875
- b_proj: float32 [4096], replicated, may hold values from -3 to 3
- norm_gain: float32 [1, 4096], replicated, may hold values from 0.1 to 1.9
- w_qkv: bfloat16 [1, 4096, 8, 512], P(None, 'dp', 'mp'), may hold values from -0.375 to 0.375
- w_out: bfloat16 [1, 8, 256, 4096], P(None, 'mp', None, 'dp'), may hold values from -0.125 to 0.125
Outputs:
- hidden_out: bfloat16 [32, 256, 4096], P('dp', 'mp')
Inputs may be any that keep to these rules, and one draw needn't show every extreme that they name: `tile_dest`: each language-model rank receives exactly 4 tiles; one source rank sends at most 2 tiles to one language-model rank, and every source rank sends 2 to some rank.
All inputs are finite; a program needn't handle non-finite values.
Results may differ from a plain program's by a relative error of at most 0.01.
Values may be sent and summed in bfloat16 or wider, within the bound.
A program may use at most 128 MiB of HBM per device.

v0:
```python
import math
import jax
import jax.numpy as jnp
from jax import lax
from jax.sharding import PartitionSpec as P

HS = 128
GROUP = 2
CAP = 2
rope_base = 500000.0
epsilon = 1e-05


def tile_angles(tile_size, head_size):
    half_size = head_size // 2
    inverse = jnp.exp(
        -(2.0 * jnp.arange(half_size, dtype=jnp.float32) / head_size) * math.log(rope_base)
    )
    positions = jnp.arange(tile_size, dtype=jnp.float32)
    return positions[:, None] * inverse[None, :]


def rotate_half(values, angles):
    half_size = values.shape[-1] // 2
    cosine = jnp.cos(angles)
    sine_part = jnp.sin(angles)
    first_half = values[..., :half_size]
    second = values[..., half_size:]
    return jnp.concatenate(
        [first_half * cosine - second * sine_part, second * cosine + first_half * sine_part],
        axis=-1,
    )


def slot_table(full_dest, dest_ids):
    full_hot = (full_dest[:, None] == dest_ids[None, :]).astype(jnp.int32)
    return jnp.sum((jnp.cumsum(full_hot, axis=0) - full_hot) * full_hot, axis=1)


def send_capped(vit_features, tile_dest, own_before, full_dest, full_slots, rank_count, my_rank):
    image_count, local_rows, vision_width = vit_features.shape
    targets = tile_dest * CAP + own_before
    placing = (targets[:, None] == jnp.arange(rank_count * CAP, dtype=jnp.int32)[None, :]).astype(
        jnp.bfloat16
    )
    flat_rows = vit_features.reshape(image_count, local_rows * vision_width)
    outgoing = jnp.dot(placing.T, flat_rows, preferred_element_type=jnp.float32).astype(
        jnp.bfloat16
    )
    outgoing = outgoing.reshape(rank_count, CAP, local_rows, vision_width)
    incoming = lax.all_to_all(outgoing, "dp", split_axis=0, concat_axis=0, tiled=True)
    image_total = full_dest.shape[0]
    dest_ids = jnp.arange(rank_count, dtype=jnp.int32)
    by_source = full_dest.reshape(rank_count, image_count)
    source_hot = (by_source[:, :, None] == dest_ids[None, None, :]).astype(jnp.int32)
    source_before = jnp.sum(
        (jnp.cumsum(source_hot, axis=1) - source_hot) * source_hot, axis=2
    ).reshape(image_total)
    columns = jnp.arange(image_total, dtype=jnp.int32) // image_count * CAP + source_before
    mine_mask = full_dest == my_rank
    pick_rows = (
        mine_mask[None, :]
        & (full_slots[None, :] == jnp.arange(image_count, dtype=jnp.int32)[:, None])
    ).astype(jnp.bfloat16)
    pick_cols = (columns[:, None] == jnp.arange(rank_count * CAP, dtype=jnp.int32)[None, :]).astype(
        jnp.bfloat16
    )
    selector = jnp.dot(pick_rows, pick_cols, preferred_element_type=jnp.float32).astype(
        jnp.bfloat16
    )
    arrived = jnp.dot(
        selector,
        incoming.reshape(rank_count * CAP, local_rows * vision_width),
        preferred_element_type=jnp.float32,
    )
    return arrived.astype(jnp.bfloat16).reshape(image_count, local_rows, vision_width)


def layer_step(hidden, gain_row, weights_qkv, weights_out, lengths, angles):
    as_float = hidden.astype(jnp.float32)
    mean_square = jnp.mean(as_float * as_float, axis=-1, keepdims=True)
    normed = (as_float * lax.rsqrt(mean_square + epsilon) * gain_row).astype(jnp.bfloat16)
    full_rows = lax.all_gather(normed, "mp", axis=1, tiled=True)
    image_count, tile_size, model_width = full_rows.shape
    head_count = weights_qkv.shape[1]
    joined_rows = jnp.dot(
        full_rows.reshape(image_count * tile_size, model_width),
        weights_qkv.reshape(model_width, -1),
        preferred_element_type=jnp.float32,
    )
    joined_rows = joined_rows.reshape(image_count, tile_size, head_count, GROUP + 2, HS)
    queries = rotate_half(joined_rows[:, :, :, :GROUP, :], angles[None, :, None, None, :]).astype(
        jnp.bfloat16
    )
    key_heads = rotate_half(joined_rows[:, :, :, GROUP, :], angles[None, :, None, :]).astype(
        jnp.bfloat16
    )
    value_heads = joined_rows[:, :, :, GROUP + 1, :].astype(jnp.bfloat16)
    score_scale = 1.0 / math.sqrt(HS)
    scores = (
        jnp.einsum("brhge,bche->bhgrc", queries, key_heads, preferred_element_type=jnp.float32)
        * score_scale
    )
    row_ids = jnp.arange(tile_size, dtype=jnp.int32)[:, None]
    col_ids = jnp.arange(tile_size, dtype=jnp.int32)[None, :]
    allowed = (col_ids <= row_ids)[None, None, None, :, :] & (
        col_ids[None, None, None, :, :] < lengths[:, None, None, None, None]
    )
    scores = jnp.where(allowed, scores, -1e30)
    row_max = jnp.max(scores, axis=-1, keepdims=True)
    weights = jnp.where(allowed, jnp.exp(scores - row_max), 0.0)
    probabilities = (weights / jnp.sum(weights, axis=-1, keepdims=True)).astype(jnp.bfloat16)
    attended = jnp.einsum(
        "bhgrc,bche->brhge", probabilities, value_heads, preferred_element_type=jnp.float32
    ).astype(jnp.bfloat16)
    head_term = jnp.dot(
        attended.reshape(image_count * tile_size, -1),
        weights_out.reshape(-1, model_width),
        preferred_element_type=jnp.float32,
    )
    head_term = head_term.reshape(image_count, tile_size, model_width)
    summed = lax.psum_scatter(
        head_term.astype(jnp.bfloat16), "mp", scatter_dimension=1, tiled=True
    ).astype(jnp.float32)
    return (as_float + summed).astype(jnp.bfloat16)


def body(
    vit_features,
    patch_counts,
    text_counts,
    tile_dest,
    text_embeds,
    w_proj,
    b_proj,
    norm_gain,
    w_qkv,
    w_out,
):
    rank_count = lax.axis_size("dp")
    my_rank = lax.axis_index("dp")
    image_count, local_rows, vision_width = vit_features.shape
    dest_ids = jnp.arange(rank_count, dtype=jnp.int32)
    own_hot = (tile_dest[:, None] == dest_ids[None, :]).astype(jnp.int32)
    own_before = jnp.sum((jnp.cumsum(own_hot, axis=0) - own_hot) * own_hot, axis=1)
    full_dest = lax.all_gather(tile_dest, "dp", axis=0, tiled=True)
    full_slots = slot_table(full_dest, dest_ids)
    arrived = send_capped(
        vit_features, tile_dest, own_before, full_dest, full_slots, rank_count, my_rank
    )
    mp_rank = lax.axis_index("mp")
    projected = (
        jnp.dot(
            arrived.reshape(image_count * local_rows, vision_width),
            w_proj,
            preferred_element_type=jnp.float32,
        )
        + b_proj
    )
    projected = projected.reshape(image_count, local_rows, -1)
    row_ids = (mp_rank * local_rows + jnp.arange(local_rows, dtype=jnp.int32))[None, :, None]
    image_end = patch_counts[:, None, None]
    text_end = (patch_counts + text_counts)[:, None, None]
    hidden = jnp.where(
        row_ids < image_end,
        projected,
        jnp.where(row_ids < text_end, text_embeds.astype(jnp.float32), 0.0),
    ).astype(jnp.bfloat16)
    lengths = patch_counts + text_counts
    all_qkv, all_out = (
        lax.all_gather(w_qkv, "dp", axis=1, tiled=True),
        lax.all_gather(w_out, "dp", axis=3, tiled=True),
    )
    tile_size = local_rows * lax.axis_size("mp")
    angles = tile_angles(tile_size, HS)
    hidden = layer_step(hidden, norm_gain[0], all_qkv[0], all_out[0], lengths, angles)
    return hidden


def solution(mesh):
    in_specs = (
        P("dp", "mp", None),
        P("dp"),
        P("dp"),
        P("dp"),
        P("dp", "mp", None),
        P(),
        P(),
        P(),
        P(None, "dp", "mp", None),
        P(None, "mp", None, "dp"),
    )
    out_specs = P("dp", "mp", None)
    return jax.shard_map(body, mesh=mesh, in_specs=in_specs, out_specs=out_specs, check_vma=False)
```

profile of v0, /device:TPU:0, one launch (start us, length us, event | category | flops | bytes accessed | tf_op | source)
XLA Modules:
  0.0 441.3 jit_solution(15001125741120260117)
XLA Ops:
  6.5 0.7 all-gather.6.cloned.1.call-update
  7.3 1.4 copy.44
  8.7 0.7 fusion.29
  9.5 0.8 select_reduce_fusion.1
  11.0 0.9 convolution_convert_fusion
  11.9 2.5 copy.45
  14.4 5.2 %all-to-all-start = ((bf16[8,2,64,1024]{3,2,1,0:T(8,128)(2,1)}), bf16[8,2,64,1024]{3,2,1,0:T(8,128)(2,1)S(1)}, u32[]{:S(2)}, u32[]{:S(2)}) async-start(bf16[8,2,64,1024]{3,2,1,0:T(8,128)(2,1)} %bitcast.63), calls=%async_computation | async-start | bytes 4194304 | tf_op jit(solution)/shard_map/all_to_all | solution.py:51
  21.0 38.3 %all-reduce = s32[32]{0:T(128)S(1)} all-reduce(s32[32]{0:T(128)S(1)} %dynamic-update-slice), channel_id=1, replica_groups=mesh['dp'=8,'mp'=4] {'dp'}, use_global_device_ids=true, to_apply=%add | all-reduce | flops 32 | bytes 256
  60.3 2.6 copy.46
  62.9 2.8 convolution_convert_fusion.1
  66.2 5.9 %convolution_add_fusion = bf16[256,4096]{1,0:T(8,128)(2,1)S(1)} fusion(bf16[256,1024]{1,0:T(8,128)(2,1)S(1)} %reshape_reshape.3, bf16[1024,4096]{1,0:T(8,128)(2,1)} %param.15, f32[4096]{0:T(1024)S(1)} %copy-done.4), kind=kOutput, calls=%fused_computation.9 | convolution fusion | flops 2149580800 | bytes 11026432 | tf_op jit(solution)/shard_map/dot_general | solution.py:153
  72.1 1.0 fusion.3
  73.2 2.0 fusion.5
  75.2 0.7 all-gather.8.cloned.1.call-update
  76.7 12.0 %all-gather.6.cloned.1.call-done = bf16[1,4096,2,512]{3,2,0,1:T(2,128)(2,1)} async-done(((bf16[1,512,2,512]{3,2,0,1:T(2,128)(2,1)}), bf16[1,4096,2,512]{3,2,0,1:T(2,128)(2,1)}) %all-gather.6.cloned.1.call-update) | async-done | bytes 8388624 | tf_op jit(solution)/shard_map/all_gather | solution.py:171
  88.7 21.5 %copy.41 = bf16[1,4096,2,512]{1,3,2,0:T(8,128)(2,1)} copy(bf16[1,4096,2,512]{3,2,0,1:T(2,128)(2,1)} %all-gather.6.cloned.1.call-done) | data formatting | bytes 16777216 | tf_op jit(solution)/shard_map/reshape;squeeze | solution.py:88
  110.2 129.7 %all-gather.4.cloned.1.call-done = bf16[4,256,4096]{2,1,0:T(8,128)(2,1)} async-done(((bf16[4,64,4096]{2,1,0:T(8,128)(2,1)}), bf16[4,256,4096]{2,1,0:T(8,128)(2,1)}) %all-gather.4.cloned.1.call-update) | async-done | bytes 8388624 | tf_op jit(solution)/shard_map/all_gather | solution.py:83
  239.9 12.7 %fusion.1 = f32[4,256,2,4,128]{1,4,3,2,0:T(8,128)S(1)} fusion(bf16[2,4,128,4096,1]{3,2,1,0,4:T(8,128)(2,1)} %bitcast.61, bf16[4,256,4096]{2,1,0:T(8,128)(2,1)} %all-gather.4.cloned.1.call-done), kind=kOutput, calls=%fused_computation.3 | convolution fusion | flops 8589934592 | bytes 20971520 | tf_op jit(solution)/shard_map/dot_general | solution.py:86
  253.2 0.8 fusion.14
  254.0 1.7 fusion.44
  256.2 21.1 %all-gather.8.cloned.1.call-done = bf16[1,2,256,4096]{3,2,1,0:T(8,128)(2,1)} async-done(((bf16[1,2,256,512]{3,2,1,0:T(8,128)(2,1)}), bf16[1,2,256,4096]{3,2,1,0:T(8,128)(2,1)}) %all-gather.8.cloned.1.call-update) | async-done | bytes 4194320 | tf_op jit(solution)/shard_map/all_gather | solution.py:172
  277.4 8.9 %convolution_convert_fusion.2 = bf16[4,256,4096]{2,1,0:T(8,128)(2,1)} fusion(bf16[4,256,512]{1,2,0:T(8,128)(2,1)S(1)} %bitcast.72, bf16[512,4096,1]{1,0,2:T(8,128)(2,1)} %bitcast.71), kind=kOutput, calls=%fused_computation.5 | convolution fusion | flops 4299161600 | bytes 13631488 | tf_op jit(solution)/shard_map/dot_general | solution.py:116
  286.3 144.8 %reduce-scatter.2.cloned.1.call-done = bf16[4,64,4096]{2,1,0:T(8,128)(2,1)} async-done(((bf16[4,256,4096]{2,1,0:T(8,128)(2,1)}), bf16[4,64,4096]{2,1,0:T(8,128)(2,1)}) %reduce-scatter.2.cloned.1.call-update) | async-done | bytes 2097168 | tf_op jit(solution)/shard_map/reduce_scatter | solution.py:122
  431.1 3.7 fusion.6
  (50 shorter events, 5.0 us)
Async XLA Ops:
  6.5 82.2 %all-gather.6.cloned.1.call-start = ((), (), s32[]{:S(2)}) async-start(), calls=%async_computation.3 | async-start | bytes 9437184 | tf_op jit(solution)/shard_map/all_gather | solution.py:171
  11.8 7.8 %copy-start.6 = (u32[32]{0:T(128)S(1)}, u32[32]{0:T(128)}, u32[]{:S(2)}) copy-start(u32[32]{0:T(128)} %constant.73) | copy-start | bytes 388
  11.8 8.9 %copy-start.2 = (s32[4]{0:T(128)S(1)}, s32[4]{0:T(128)}, u32[]{:S(2)}) copy-start(s32[4]{0:T(128)} %param.13) | copy-start | bytes 52
  11.9 48.1 %copy-start.3 = (s32[4]{0:T(128)S(1)}, s32[4]{0:T(128)}, u32[]{:S(2)}) copy-start(s32[4]{0:T(128)} %param.11) | copy-start | bytes 52
  11.9 48.1 %copy-start.5 = (s32[4]{0:T(128)S(1)}, s32[4]{0:T(128)}, u32[]{:S(2)}) copy-start(s32[4]{0:T(128)} %param.12) | copy-start | bytes 52
  14.4 46.0 %all-to-all-start = ((bf16[8,2,64,1024]{3,2,1,0:T(8,128)(2,1)}), bf16[8,2,64,1024]{3,2,1,0:T(8,128)(2,1)S(1)}, u32[]{:S(2)}, u32[]{:S(2)}) async-start(bf16[8,2,64,1024]{3,2,1,0:T(8,128)(2,1)} %bitcast.63), calls=%async_computation | async-start | bytes 4194304 | tf_op jit(solution)/shard_map/all_to_all | solution.py:51
  19.6 46.6 %copy-start.4 = (f32[4096]{0:T(1024)S(1)}, f32[4096]{0:T(1024)}, u32[]{:S(2)}) copy-start(f32[4096]{0:T(1024)} %param.16) | copy-start | bytes 49156
  19.6 220.3 %all-gather.4.cloned.1.call-start = ((), (), s32[]{:S(2)}) async-start(), calls=%async_computation.2 | async-start | bytes 10485760 | tf_op jit(solution)/shard_map/all_gather | solution.py:83
  66.1 5.9 %copy-start = (bf16[4,64,4096]{2,1,0:T(8,128)(2,1)S(1)}, bf16[4,64,4096]{2,1,0:T(8,128)(2,1)}, u32[]{:S(2)}) copy-start(bf16[4,64,4096]{2,1,0:T(8,128)(2,1)} %param.14) | copy-start | bytes 6291460
  72.1 1.1 copy-start.1
  75.1 202.2 %all-gather.8.cloned.1.call-start = ((), (), s32[]{:S(2)}) async-start(), calls=%async_computation.4 | async-start | bytes 4718592 | tf_op jit(solution)/shard_map/all_gather | solution.py:172
  75.9 355.2 %reduce-scatter.2.cloned.1.call-start = ((), (), s32[]{:S(2)}) async-start(), calls=%async_computation.5 | async-start | bytes 10485760 | tf_op jit(solution)/shard_map/reduce_scatter | solution.py:122
Sparse Core Ops, SparseCore 0:
  9.2 79.4 all-gather.5
  90.3 149.5 all-gather.3
  241.8 35.5 all-gather.7
  286.4 144.6 reduce-scatter.1
where the time goes:
time: 442 us; the launch traced here: 441 us
  waiting for transfers between devices  309 us (70%)
  blocking collectives  38.3 us (9%)
  matrix products  32.5 us (7%)
  local copies, waits for them, and re-layouts  29.7 us (7%)
  between operations  13.9 us (3%)
  other arithmetic  12.4 us (3%)
  starting transfers between devices  5.51 us (1%)
    reduce_scatter x1, waiting for transfers between devices, layer_step(): lax.psum_scatter(head_term.astype(jnp.bfloat16), 'mp', scatter_dimension=...  145 us
    all_gather x1, waiting for transfers between devices, layer_step(): full_rows = lax.all_gather(normed, 'mp', axis=1, tiled=True)  130 us
    unnamed x1, blocking collectives  38.3 us
    another operation x1, local copies, waits for them, and re-layouts, layer_step(): weights_qkv.reshape(model_width, -1)  21.5 us
    all_gather x1, waiting for transfers between devices, body(): lax.all_gather(w_out, 'dp', axis=3, tiled=True)  21.1 us
    dot_general x1, matrix products, layer_step(): jnp.dot(full_rows.reshape(image_count * tile_size, model_width), weights_...  12.7 us
    all_gather x1, waiting for transfers between devices, body(): lax.all_gather(w_qkv, 'dp', axis=1, tiled=True)  12 us
    dot_general x1, matrix products, layer_step(): jnp.dot(attended.reshape(image_count * tile_size, -1), weights_out.reshap...  8.92 us
  transfers between devices with their start and end apart: 5, of which 4 were waited for; matrix products, arithmetic and copies ran while one was open for 14% of the time, Pallas kernels for 0%

commit v1 on v0

--- a/solution.py
+++ b/solution.py
@@ -80,7 +80,10 @@
     as_float = hidden.astype(jnp.float32)
     mean_square = jnp.mean(as_float * as_float, axis=-1, keepdims=True)
     normed = (as_float * lax.rsqrt(mean_square + epsilon) * gain_row).astype(jnp.bfloat16)
-    full_rows = lax.all_gather(normed, "mp", axis=1, tiled=True)
+    _finish_leaf = lambda field, d_out: jnp.concatenate(
+        lax.all_gather(field, axis_name="mp"), d_out
+    )
+    full_rows = _finish_leaf(normed, 1)
     image_count, tile_size, model_width = full_rows.shape
     head_count = weights_qkv.shape[1]
     joined_rows = jnp.dot(

time: 442 us -> 470 us (1.063)
  waiting for transfers between devices: 309 us -> 341 us
  blocking collectives: 38.3 us -> 27.2 us
  local copies, waits for them, and re-layouts: 29.7 us -> 37.3 us
    all_gather x1, waiting for transfers between devices: 12 us -> 46.4 us  [body(): lax.all_gather(w_qkv, 'dp', axis=1, tiled=True)]
    all_gather x1, waiting for transfers between devices: 21.1 us -> 1.28 us  [body(): lax.all_gather(w_out, 'dp', axis=3, tiled=True)]
    all_gather x1, waiting for transfers between devices: 130 us -> 147 us  [layer_step(): lax.all_gather(field, axis_name='mp')]
    unnamed x1, blocking collectives: 38.3 us -> 27.2 us
    all_gather x0 -> x1, local copies, waits for them, and re-layouts: none -> 7.96 us  [layer_step(): lax.all_gather(field, axis_name='mp')]
  transfers between devices with their start and end apart: 5 -> 5, of which waited for: 4 -> 4; matrix products, arithmetic and copies ran while one was open for 14% -> 10% of each run, Pallas kernels for 0% -> 0%
where the time goes in v1:
time: 470 us
  waiting for transfers between devices  341 us (73%)
  local copies, waits for them, and re-layouts  37.3 us (8%)
  matrix products  32.3 us (7%)
  blocking collectives  27.2 us (6%)
  between operations  14.1 us (3%)
  other arithmetic  12.4 us (3%)
  starting transfers between devices  5.53 us (1%)
    all_gather x1, waiting for transfers between devices, layer_step(): lax.all_gather(field, axis_name='mp')  147 us
    reduce_scatter x1, waiting for transfers between devices, layer_step(): lax.psum_scatter(head_term.astype(jnp.bfloat16), 'mp', scatter_dimension=...  145 us
    all_gather x1, waiting for transfers between devices, body(): lax.all_gather(w_qkv, 'dp', axis=1, tiled=True)  46.4 us
    unnamed x1, blocking collectives  27.2 us
    another operation x1, local copies, waits for them, and re-layouts, layer_step(): weights_qkv.reshape(model_width, -1)  21.2 us
    dot_general x1, matrix products, layer_step(): jnp.dot(full_rows.reshape(image_count * tile_size, model_width), weights_...  13.2 us
  transfers between devices with their start and end apart: 5, of which 4 were waited for; matrix products, arithmetic and copies ran while one was open for 10% of the time, Pallas kernels for 0%

profile of v1, /device:TPU:0, one launch (start us, length us, event | category | flops | bytes accessed | tf_op | source)
XLA Modules:
  0.0 469.5 jit_solution(337209637453096029)
XLA Ops:
  6.5 1.4 copy.48
  8.0 0.7 fusion.27
  8.8 0.8 select_reduce_fusion.1
  10.3 0.9 convolution_convert_fusion
  11.2 2.5 copy.49
  13.6 5.2 %all-to-all-start = ((bf16[8,2,64,1024]{3,2,1,0:T(8,128)(2,1)}), bf16[8,2,64,1024]{3,2,1,0:T(8,128)(2,1)S(1)}, u32[]{:S(2)}, u32[]{:S(2)}) async-start(bf16[8,2,64,1024]{3,2,1,0:T(8,128)(2,1)} %bitcast.69), calls=%async_computation | async-start | bytes 4194304 | tf_op jit(solution)/shard_map/all_to_all | solution.py:51
  20.5 27.2 %all-reduce = s32[32]{0:T(128)S(1)} all-reduce(s32[32]{0:T(128)S(1)} %dynamic-update-slice), channel_id=1, replica_groups=mesh['dp'=8,'mp'=4] {'dp'}, use_global_device_ids=true, to_apply=%add | all-reduce | flops 32 | bytes 256
  48.7 2.5 copy.50
  51.2 2.2 convolution_convert_fusion.1
  53.8 5.9 %convolution_add_fusion = bf16[256,4096]{1,0:T(8,128)(2,1)S(1)} fusion(bf16[256,1024]{1,0:T(8,128)(2,1)S(1)} %reshape_reshape.4, bf16[1024,4096]{1,0:T(8,128)(2,1)} %param.15, f32[4096]{0:T(1024)S(1)} %copy-done.4), kind=kOutput, calls=%fused_computation.7 | convolution fusion | flops 2149580800 | bytes 11026432 | tf_op jit(solution)/shard_map/dot_general | solution.py:156
  59.7 1.0 fusion.1
  60.8 2.0 fusion.3
  62.8 0.7 all-gather.5.cloned.1.call-update
  65.1 146.8 %all-gather.9.cloned.1.call-done = bf16[16,64,4096]{2,1,0:T(8,128)(2,1)} async-done(((bf16[4,64,4096]{2,1,0:T(8,128)(2,1)}), bf16[16,64,4096]{2,1,0:T(8,128)(2,1)}) %all-gather.9.cloned.1.call-update) | async-done | bytes 8388624 | tf_op jit(solution)/shard_map/all_gather | solution.py:84
  212.0 8.0 %copy.32 = bf16[4,4,64,4096]{3,2,0,1:T(8,128)(2,1)} copy(bf16[4,4,64,4096]{3,2,1,0:T(8,128)(2,1)} %bitcast.65) | data formatting | bytes 16777216 | tf_op jit(solution)/shard_map/all_gather | solution.py:84
  219.9 46.4 %all-gather.5.cloned.1.call-done = bf16[1,4096,2,512]{3,2,0,1:T(2,128)(2,1)} async-done(((bf16[1,512,2,512]{3,2,0,1:T(2,128)(2,1)}), bf16[1,4096,2,512]{3,2,0,1:T(2,128)(2,1)}) %all-gather.5.cloned.1.call-update) | async-done | bytes 8388624 | tf_op jit(solution)/shard_map/all_gather | solution.py:174
  266.3 21.2 %copy.45 = bf16[1,4096,2,512]{1,3,2,0:T(8,128)(2,1)} copy(bf16[1,4096,2,512]{3,2,0,1:T(2,128)(2,1)} %all-gather.5.cloned.1.call-done) | data formatting | bytes 16777216 | tf_op jit(solution)/shard_map/reshape;squeeze | solution.py:91
  287.5 13.2 %fusion.43 = f32[4,256,2,4,128]{1,4,3,2,0:T(8,128)S(1)} fusion(bf16[4,256,4096,1,1]{2,1,4,3,0:T(8,128)(2,1)} %bitcast.66, bf16[2,4,128,4096,1]{3,2,1,0,4:T(8,128)(2,1)} %bitcast.67), kind=kOutput, calls=%fused_computation.80 | convolution fusion | flops 8589934592 | bytes 20971520 | tf_op jit(solution)/shard_map/dot_general | solution.py:89
  301.3 0.8 fusion.12
  302.1 1.7 fusion.42
  304.3 1.3 all-gather.7.cloned.1.call-done
  305.6 8.9 %convolution_convert_fusion.2 = bf16[4,256,4096]{2,1,0:T(8,128)(2,1)} fusion(bf16[4,256,512]{1,2,0:T(8,128)(2,1)S(1)} %bitcast.78, bf16[512,4096,1]{1,0,2:T(8,128)(2,1)} %bitcast.77), kind=kOutput, calls=%fused_computation.3 | convolution fusion | flops 4299161600 | bytes 13631488 | tf_op jit(solution)/shard_map/dot_general | solution.py:119
  314.5 144.8 %reduce-scatter.2.cloned.1.call-done = bf16[4,64,4096]{2,1,0:T(8,128)(2,1)} async-done(((bf16[4,256,4096]{2,1,0:T(8,128)(2,1)}), bf16[4,64,4096]{2,1,0:T(8,128)(2,1)}) %reduce-scatter.2.cloned.1.call-update) | async-done | bytes 2097168 | tf_op jit(solution)/shard_map/reduce_scatter | solution.py:125
  459.3 3.7 fusion.4
  (51 shorter events, 5.8 us)
Async XLA Ops:
  11.1 7.8 %copy-start.6 = (u32[32]{0:T(128)S(1)}, u32[32]{0:T(128)}, u32[]{:S(2)}) copy-start(u32[32]{0:T(128)} %constant.73) | copy-start | bytes 388
  11.1 9.2 %copy-start.2 = (s32[4]{0:T(128)S(1)}, s32[4]{0:T(128)}, u32[]{:S(2)}) copy-start(s32[4]{0:T(128)} %param.13) | copy-start | bytes 52
  11.1 37.2 %copy-start.3 = (s32[4]{0:T(128)S(1)}, s32[4]{0:T(128)}, u32[]{:S(2)}) copy-start(s32[4]{0:T(128)} %param.11) | copy-start | bytes 52
  11.2 37.2 %copy-start.5 = (s32[4]{0:T(128)S(1)}, s32[4]{0:T(128)}, u32[]{:S(2)}) copy-start(s32[4]{0:T(128)} %param.12) | copy-start | bytes 52
  13.6 35.1 %all-to-all-start = ((bf16[8,2,64,1024]{3,2,1,0:T(8,128)(2,1)}), bf16[8,2,64,1024]{3,2,1,0:T(8,128)(2,1)S(1)}, u32[]{:S(2)}, u32[]{:S(2)}) async-start(bf16[8,2,64,1024]{3,2,1,0:T(8,128)(2,1)} %bitcast.69), calls=%async_computation | async-start | bytes 4194304 | tf_op jit(solution)/shard_map/all_to_all | solution.py:51
  18.8 35.0 %copy-start.4 = (f32[4096]{0:T(1024)S(1)}, f32[4096]{0:T(1024)}, u32[]{:S(2)}) copy-start(f32[4096]{0:T(1024)} %param.16) | copy-start | bytes 49156
  18.8 193.1 %all-gather.9.cloned.1.call-start = ((), (), s32[]{:S(2)}) async-start(), calls=%async_computation.5 | async-start | bytes 10485760 | tf_op jit(solution)/shard_map/all_gather | solution.py:84
  53.8 5.9 %copy-start = (bf16[4,64,4096]{2,1,0:T(8,128)(2,1)S(1)}, bf16[4,64,4096]{2,1,0:T(8,128)(2,1)}, u32[]{:S(2)}) copy-start(bf16[4,64,4096]{2,1,0:T(8,128)(2,1)} %param.14) | copy-start | bytes 6291460
  59.7 1.1 copy-start.1
  62.8 203.5 %all-gather.5.cloned.1.call-start = ((), (), s32[]{:S(2)}) async-start(), calls=%async_computation.2 | async-start | bytes 9437184 | tf_op jit(solution)/shard_map/all_gather | solution.py:174
  63.5 242.1 %all-gather.7.cloned.1.call-start = ((), (), s32[]{:S(2)}) async-start(), calls=%async_computation.3 | async-start | bytes 4718592 | tf_op jit(solution)/shard_map/all_gather | solution.py:175
  64.3 395.0 %reduce-scatter.2.cloned.1.call-start = ((), (), s32[]{:S(2)}) async-start(), calls=%async_computation.4 | async-start | bytes 10485760 | tf_op jit(solution)/shard_map/reduce_scatter | solution.py:125
Sparse Core Ops, SparseCore 0:
  62.9 149.0 all-gather.8
  213.8 52.4 all-gather.4
  268.2 37.3 all-gather.6
  314.7 144.6 reduce-scatter.1
